TPU v7x, 32 devices: a whole 2x2x4 slice. The times are simulated.
32 devices in a mesh: dp: 2 (over x), section: 4 (over y, core), tensor: 4 (over z).
Axes of the slice: x: 2, y: 2, z: 4, core: 2. Of those that a mesh axis runs over, the one named last changes fastest.
Arguments:
- failed_section: int32 [2], P('dp'), may hold values from 0 to 999
- token_ids: int32 [2, 2048], P('dp'), may hold values from 0 to 100001, as said below
- section_outputs: bfloat16 [2, 4, 2048, 2048], P('dp', 'section', None, 'tensor'), may hold values from -11 to 11
- w_query: float32 [4, 2048, 1024], P('section', 'dp', 'tensor'), may hold values from -1 to 1
- w_key: float32 [4, 2048, 1024], P('section', 'dp', 'tensor'), may hold values from -2 to 2
- w_value: float32 [4, 2048, 1024], P('section', 'dp', 'tensor'), may hold values from -0.125 to 0.125
- w_out: float32 [4, 2048, 1024], P('section', 'dp', 'tensor'), may hold values from -0.75 to 0.75
- m_value: float32 [4, 2048, 1024], P('section', 'dp', 'tensor'), may hold values from -3 to 3
- v_value: float32 [4, 2048, 1024], P('section', 'dp', 'tensor'), may hold values from 0.001 to 1
- m_out: float32 [4, 2048, 1024], P('section', 'dp', 'tensor'), may hold values from -3 to 3
- v_out: float32 [4, 2048, 1024], P('section', 'dp', 'tensor'), may hold values from 0.001 to 1
Outputs:
- restored_query: float32 [2, 4, 2048, 1024], P('dp', 'section', None, 'tensor')
- restored_key: float32 [2, 4, 2048, 1024], P('dp', 'section', None, 'tensor')
- restored_value: float32 [2, 4, 2048, 1024], P('dp', 'section', None, 'tensor')
- restored_out: float32 [2, 4, 2048, 1024], P('dp', 'section', None, 'tensor')
- restored_m_value: float32 [2, 4, 2048, 1024], P('dp', 'section', None, 'tensor')
- restored_v_value: float32 [2, 4, 2048, 1024], P('dp', 'section', None, 'tensor')
- restored_m_out: float32 [2, 4, 2048, 1024], P('dp', 'section', None, 'tensor')
- restored_v_out: float32 [2, 4, 2048, 1024], P('dp', 'section', None, 'tensor')
- attn_update: bfloat16 [2, 4, 2048, 2048], P('dp', 'section', None, 'tensor')
Inputs may be any that keep to these rules, and one draw needn't show every extreme that they name: `token_ids`: token ids of each replica's micro-batch; the id 100001 ends a document, the others are ordinary tokens below 100000.
All inputs are finite; a program needn't handle non-finite values.
Results may differ from a plain program's by a relative error of at most 0.0087.
Values may be sent and summed in bfloat16 or wider, within the bound.
A program may use at most 128 MiB of HBM per device.

v0:
```python
import math
import jax
import jax.numpy as jnp
from jax import lax
from jax.sharding import PartitionSpec as P

HD = 128
end_token = 100001
mask_fill = -1e30


def passed_along(array, axis, by):
    count = lax.axis_size(axis)
    return lax.ppermute(array, axis, [(i, (i + by) % count) for i in range(count)])


def document_ids(token_row):
    doc_ends = (token_row == end_token).astype(jnp.int32)
    return jnp.cumsum(doc_ends) - doc_ends


def attend(queries, key_vals, value_vals, token_row):
    token_count = queries.shape[0]
    heads_local = queries.shape[1] // HD
    block_rows = min(512, token_count)
    document = document_ids(token_row)
    positions = jnp.arange(token_count, dtype=jnp.int32)
    key_heads = key_vals.reshape(token_count, heads_local, HD)
    value_heads = value_vals.reshape(token_count, heads_local, HD)

    def one_block(block_index):
        first_row = block_index * block_rows
        query_block = lax.dynamic_slice_in_dim(queries, first_row, block_rows, 0).reshape(
            block_rows, heads_local, HD
        )
        scores = jnp.einsum(
            "qhd,khd->hqk", query_block, key_heads, preferred_element_type=jnp.float32
        ) * (1.0 / math.sqrt(HD))
        query_pos = lax.dynamic_slice_in_dim(positions, first_row, block_rows, 0)
        query_doc = lax.dynamic_slice_in_dim(document, first_row, block_rows, 0)
        allowed = (positions[None, :] <= query_pos[:, None]) & (
            document[None, :] == query_doc[:, None]
        )
        scores = jnp.where(allowed[None], scores, mask_fill)
        highest = jnp.max(scores, axis=2, keepdims=True)
        weights = jnp.exp(scores - highest)
        probs = (weights / jnp.sum(weights, axis=2, keepdims=True)).astype(jnp.bfloat16)
        context = jnp.einsum(
            "hqk,khd->qhd", probs, value_heads, preferred_element_type=jnp.float32
        ).astype(jnp.bfloat16)
        return context.reshape(block_rows, heads_local * HD)

    blocks = lax.map(one_block, jnp.arange(token_count // block_rows, dtype=jnp.int32))
    return blocks.reshape(token_count, heads_local * HD)


def shards(
    failed_section,
    token_ids,
    section_outputs,
    w_query,
    w_key,
    w_value,
    w_out,
    m_value,
    v_value,
    m_out,
    v_out,
):
    section_failed = jnp.remainder(failed_section[0], lax.axis_size("section"))
    replacing = lax.axis_index("section") == section_failed
    states = (
        lax.all_gather(w_query, "dp", axis=1, tiled=True),
        lax.all_gather(w_key, "dp", axis=1, tiled=True),
        lax.all_gather(w_value, "dp", axis=1, tiled=True),
        lax.all_gather(w_out, "dp", axis=1, tiled=True),
        lax.all_gather(m_value, "dp", axis=1, tiled=True),
        lax.all_gather(v_value, "dp", axis=1, tiled=True),
        lax.all_gather(m_out, "dp", axis=1, tiled=True),
        lax.all_gather(v_out, "dp", axis=1, tiled=True),
    )
    masters = states[:4]
    moments = states[4:]
    query_bf = masters[0][0].astype(jnp.bfloat16)
    key_bf = masters[1][0].astype(jnp.bfloat16)
    value_bf = masters[2][0].astype(jnp.bfloat16)
    out_bf = masters[3][0].astype(jnp.bfloat16)
    inner_local = query_bf.shape[1]
    w_joined = jnp.concatenate([query_bf, key_bf, value_bf], axis=1)
    incoming = passed_along(section_outputs, "section", 1)
    projected = jnp.dot(
        lax.all_gather(incoming, "tensor", axis=3, tiled=True)[0, 0],
        w_joined,
        preferred_element_type=jnp.float32,
    )
    queries = projected[:, :inner_local].astype(jnp.bfloat16)
    key_vals = projected[:, inner_local : 2 * inner_local].astype(jnp.bfloat16)
    value_vals = projected[:, 2 * inner_local :].astype(jnp.bfloat16)
    context = attend(queries, key_vals, value_vals, token_ids[0])
    context_whole = lax.all_gather(context, "tensor", axis=1, tiled=True)
    out_slice = lax.all_to_all(out_bf, "tensor", split_axis=0, concat_axis=1, tiled=True)
    update = lax.dot_general(
        context_whole, out_slice, (((1,), (1,)), ((), ())), preferred_element_type=jnp.float32
    ).astype(jnp.bfloat16)

    def placed(gathered):
        return jnp.where(replacing, gathered[None], jnp.zeros_like(gathered[None]))

    update_block = jnp.where(
        replacing, update[None, None], jnp.zeros((1, 1) + update.shape, jnp.bfloat16)
    )
    return (
        placed(masters[0]),
        placed(masters[1]),
        placed(masters[2]),
        placed(masters[3]),
        placed(moments[0]),
        placed(moments[1]),
        placed(moments[2]),
        placed(moments[3]),
        update_block,
    )


def solution(mesh):
    return jax.shard_map(
        shards,
        mesh=mesh,
        in_specs=(
            P("dp"),
            P("dp", None),
            P("dp", "section", None, "tensor"),
            P("section", "dp", "tensor"),
            P("section", "dp", "tensor"),
            P("section", "dp", "tensor"),
            P("section", "dp", "tensor"),
            P("section", "dp", "tensor"),
            P("section", "dp", "tensor"),
            P("section", "dp", "tensor"),
            P("section", "dp", "tensor"),
        ),
        out_specs=(
            P("dp", "section", None, "tensor"),
            P("dp", "section", None, "tensor"),
            P("dp", "section", None, "tensor"),
            P("dp", "section", None, "tensor"),
            P("dp", "section", None, "tensor"),
            P("dp", "section", None, "tensor"),
            P("dp", "section", None, "tensor"),
            P("dp", "section", None, "tensor"),
            P("dp", "section", None, "tensor"),
        ),
        check_vma=False,
    )
```

profile of v0, /device:TPU:0, one launch (start us, length us, event | category | flops | bytes accessed | tf_op | source)
XLA Modules:
  0.0 532.3 jit_solution(9929025683600086122)
XLA Ops:
  9.4 25.7 %collective-permute-done = bf16[1,1,2048,512]{3,2,1,0:T(8,128)(2,1)S(1)} collective-permute-done((bf16[1,1,2048,512]{3,2,1,0:T(8,128)(2,1)}, bf16[1,1,2048,512]{3,2,1,0:T(8,128)(2,1)S(1)}, u32[]{:S(2)}, u32[]{:S(2)}) %collective-permute-start) | collective-permute-done | bytes 2097184 | tf_op jit(solution)/shard_map/ppermute | solution.py:14
  41.2 4.2 all-gather.13.cloned.1.call-done
  45.4 3.8 convert_bitcast_fusion.1
  49.2 30.9 %all-gather.15.cloned.1.call-done = f32[1,2048,256]{2,1,0:T(8,128)} async-done(((f32[1,1024,256]{2,1,0:T(8,128)}), f32[1,2048,256]{2,1,0:T(8,128)}) %all-gather.15.cloned.1.call-update) | async-done | bytes 2097168 | tf_op jit(solution)/shard_map/all_gather | solution.py:75
  80.0 3.8 convert_bitcast_fusion
  83.8 30.9 %all-gather.11.cloned.1.call-done = f32[1,2048,256]{2,1,0:T(8,128)} async-done(((f32[1,1024,256]{2,1,0:T(8,128)}), f32[1,2048,256]{2,1,0:T(8,128)}) %all-gather.11.cloned.1.call-update) | async-done | bytes 2097168 | tf_op jit(solution)/shard_map/all_gather | solution.py:73
  114.7 4.1 convert_bitcast_fusion.2
  118.8 147.5 %all-gather.27.cloned.1.call-done = bf16[1,1,2048,2048]{3,2,1,0:T(8,128)(2,1)} async-done(((bf16[1,1,2048,512]{3,2,1,0:T(8,128)(2,1)}), bf16[1,1,2048,2048]{3,2,1,0:T(8,128)(2,1)}) %all-gather.27.cloned.1.call-update) | async-done | bytes 8388624 | tf_op jit(solution)/shard_map/all_gather | solution.py:92
  266.4 9.4 %fusion.21 = bf16[2048,768]{0,1:T(8,128)(2,1)S(1)} fusion(bf16[1,1,2048,2048]{3,2,1,0:T(8,128)(2,1)} %all-gather.27.cloned.1.call-done, bf16[2048,256]{1,0:T(8,128)(2,1)S(1)} %get-tuple-element.126, bf16[2048,256]{1,0:T(8,128)(2,1)S(1)} %get-tuple-element.124, bf16[2048,256]{1,0:T(8,128)(2,1)} %get-tuple-element.122), kind=kOutput, calls=%fused_computation.24 | convolution fusion | flops 6453460992 | bytes 14680064 | tf_op jit(solution)/shard_map/dot_general | solution.py:91
  278.4 63.1 %while.11 = (s32[]{:T(128)}, bf16[4,512,256]{2,1,0:T(8,128)(2,1)S(1)}, s32[2048]{0:T(1024)S(1)}, s32[4]{0:T(128)S(1)}, s32[2048]{0:T(1024)S(1)}, /*index=5*/bf16...) while((s32[]{:T(128)}, ...), condition=%wide.region_5.6_spmd.clone, body=%wide.region_2.5_spmd.clone.sunk | while | flops 1089603584 | bytes 23105728 | solution.py:53
  280.7 7.9 %fusion.47 = (f32[2,512]{1,0:T(2,128)S(1)}, f32[2,512,2048]{2,1,0:T(8,128)}) fusion(pred[512,2048]{1,0:T(8,128)(4,1)S(1)} %compare_and_fusion.2, bf16[512,2,128]{0,2,1:T(8,128)(2,1)S(1)} %bitcast.71, bf16[2048,2,128]{2,0,1:T(8,128)(2,1)} %get-tuple-element.211), kind=kOutput, calls=%fused_computation.43.clone.1 | convolution fusion | flops 545261568 | bytes 10752000 | tf_op jit(solution)/shard_map/while/body/eval_jaxpr/sub | solution.py:46
  288.6 5.2 fusion.48
  296.4 7.9 %fusion.47 = (f32[2,512]{1,0:T(2,128)S(1)}, f32[2,512,2048]{2,1,0:T(8,128)}) fusion(pred[512,2048]{1,0:T(8,128)(4,1)S(1)} %compare_and_fusion.2, bf16[512,2,128]{0,2,1:T(8,128)(2,1)S(1)} %bitcast.71, bf16[2048,2,128]{2,0,1:T(8,128)(2,1)} %get-tuple-element.211), kind=kOutput, calls=%fused_computation.43.clone.1 | convolution fusion | flops 545261568 | bytes 10752000 | tf_op jit(solution)/shard_map/while/body/eval_jaxpr/sub | solution.py:46
  304.2 5.7 %fusion.48 = bf16[2,512,128]{1,2,0:T(8,128)(2,1)S(1)} fusion(bf16[2048,2,128]{0,2,1:T(8,128)(2,1)} %get-tuple-element.212, f32[2,512,2048]{2,1,0:T(8,128)} %get-tuple-element.179, f32[2,512]{1,0:T(2,128)S(1)} %get-tuple-element.180), kind=kOutput, calls=%fused_computation.10.clone.1 | convolution fusion | flops 541196288 | bytes 9703424 | tf_op jit(solution)/shard_map/while/body/eval_jaxpr/hqk,khd->qhd/dot_general | solution.py:48
  312.5 7.9 %fusion.47 = (f32[2,512]{1,0:T(2,128)S(1)}, f32[2,512,2048]{2,1,0:T(8,128)}) fusion(pred[512,2048]{1,0:T(8,128)(4,1)S(1)} %compare_and_fusion.2, bf16[512,2,128]{0,2,1:T(8,128)(2,1)S(1)} %bitcast.71, bf16[2048,2,128]{2,0,1:T(8,128)(2,1)} %get-tuple-element.211), kind=kOutput, calls=%fused_computation.43.clone.1 | convolution fusion | flops 545261568 | bytes 10752000 | tf_op jit(solution)/shard_map/while/body/eval_jaxpr/sub | solution.py:46
  320.4 5.2 fusion.48
  328.2 7.9 %fusion.47 = (f32[2,512]{1,0:T(2,128)S(1)}, f32[2,512,2048]{2,1,0:T(8,128)}) fusion(pred[512,2048]{1,0:T(8,128)(4,1)S(1)} %compare_and_fusion.2, bf16[512,2,128]{0,2,1:T(8,128)(2,1)S(1)} %bitcast.71, bf16[2048,2,128]{2,0,1:T(8,128)(2,1)} %get-tuple-element.211), kind=kOutput, calls=%fused_computation.43.clone.1 | convolution fusion | flops 545261568 | bytes 10752000 | tf_op jit(solution)/shard_map/while/body/eval_jaxpr/sub | solution.py:46
  336.0 5.2 fusion.48
  342.5 4.4 fusion.31
  353.7 14.6 %all-gather.23.cloned.1.call-done = f32[1,2048,256]{2,1,0:T(8,128)} async-done(((f32[1,1024,256]{2,1,0:T(8,128)}), f32[1,2048,256]{2,1,0:T(8,128)}) %all-gather.23.cloned.1.call-update) | async-done | bytes 2097168 | tf_op jit(solution)/shard_map/all_gather | solution.py:79
  371.3 31.6 %all-gather.21.cloned.1.call-done = f32[1,2048,256]{2,1,0:T(8,128)} async-done(((f32[1,1024,256]{2,1,0:T(8,128)}), f32[1,2048,256]{2,1,0:T(8,128)}) %all-gather.21.cloned.1.call-update) | async-done | bytes 2097168 | tf_op jit(solution)/shard_map/all_gather | solution.py:78
  406.0 31.6 %all-gather.19.cloned.1.call-done = f32[1,2048,256]{2,1,0:T(8,128)} async-done(((f32[1,1024,256]{2,1,0:T(8,128)}), f32[1,2048,256]{2,1,0:T(8,128)}) %all-gather.19.cloned.1.call-update) | async-done | bytes 2097168 | tf_op jit(solution)/shard_map/all_gather | solution.py:77
  441.2 78.4 %all-gather.29.cloned.1.call-done = bf16[2048,1024]{1,0:T(8,128)(2,1)} async-done(((bf16[2048,256]{1,0:T(8,128)(2,1)}), bf16[2048,1024]{1,0:T(8,128)(2,1)}) %all-gather.29.cloned.1.call-update) | async-done | bytes 4194320 | tf_op jit(solution)/shard_map/all_gather | solution.py:100
  519.6 5.8 %fusion.27 = bf16[1,1,2048,512]{3,2,1,0:T(8,128)(2,1)} fusion(bf16[2048,1024]{1,0:T(8,128)(2,1)} %all-gather.29.cloned.1.call-done, bf16[512,1024]{0,1:T(8,128)(2,1)S(1)} %bitcast.76, pred[]{:T(512)S(6)} %eq.31), kind=kOutput, calls=%fused_computation.27 | convolution fusion | flops 2149580800 | bytes 7340033 | tf_op jit(solution)/shard_map/dot_general | solution.py:102
  (75 shorter events, 34.9 us)
Async XLA Ops:
  7.2 38.2 %all-gather.13.cloned.1.call-start = ((), (), s32[]{:S(2)}) async-start(), calls=%async_computation.2 | async-start | bytes 3145728 | tf_op jit(solution)/shard_map/all_gather | solution.py:74
  7.9 72.1 %all-gather.15.cloned.1.call-start = ((), (), s32[]{:S(2)}) async-start(), calls=%async_computation.3 | async-start | bytes 3145728 | tf_op jit(solution)/shard_map/all_gather | solution.py:75
  8.7 106.1 %all-gather.11.cloned.1.call-start = ((), (), s32[]{:S(2)}) async-start(), calls=%async_computation.1 | async-start | bytes 3145728 | tf_op jit(solution)/shard_map/all_gather | solution.py:73
  8.7 26.4 %collective-permute-start = (bf16[1,1,2048,512]{3,2,1,0:T(8,128)(2,1)}, bf16[1,1,2048,512]{3,2,1,0:T(8,128)(2,1)S(1)}, u32[]{:S(2)}, u32[]{:S(2)}) collective-permute-start(bf16[1,1,2048,512]{3,2,1,0:T(8,128)(2,1)} %param.15), channel_id=1, source_target_pairs={{0,4},{4,8},{8,12},{12,0},{1,5},{5,9},{9,13},{13,1},{2,6},{6,10},{... | collective-permute-start | bytes 6291464 | tf_op jit(solution)/shard_map/ppermute | solution.py:14
  9.4 257.0 %all-gather.27.cloned.1.call-start = ((), (), s32[]{:S(2)}) async-start(), calls=%async_computation.9 | async-start | bytes 10485760 | tf_op jit(solution)/shard_map/all_gather | solution.py:92
  35.1 1.3 copy-start
  36.5 306.0 %all-gather.17.cloned.1.call-start = ((), (), s32[]{:S(2)}) async-start(), calls=%async_computation.4 | async-start | bytes 3145728 | tf_op jit(solution)/shard_map/all_gather | solution.py:76
  37.1 3.5 copy-start.2
  37.1 313.6 %all-gather.25.cloned.1.call-start = ((), (), s32[]{:S(2)}) async-start(), calls=%async_computation.8 | async-start | bytes 3145728 | tf_op jit(solution)/shard_map/all_gather | solution.py:80
  37.6 330.6 %all-gather.23.cloned.1.call-start = ((), (), s32[]{:S(2)}) async-start(), calls=%async_computation.7 | async-start | bytes 3145728 | tf_op jit(solution)/shard_map/all_gather | solution.py:79
  38.4 364.5 %all-gather.21.cloned.1.call-start = ((), (), s32[]{:S(2)}) async-start(), calls=%async_computation.6 | async-start | bytes 3145728 | tf_op jit(solution)/shard_map/all_gather | solution.py:78
  39.1 398.5 %all-gather.19.cloned.1.call-start = ((), (), s32[]{:S(2)}) async-start(), calls=%async_computation.5 | async-start | bytes 3145728 | tf_op jit(solution)/shard_map/all_gather | solution.py:77
  39.9 479.7 %all-gather.29.cloned.1.call-start = ((), (), s32[]{:S(2)}) async-start(), calls=%async_computation.10 | async-start | bytes 5242880 | tf_op jit(solution)/shard_map/all_gather | solution.py:100
  341.4 1.0 copy-start.1
  346.9 93.7 %all-to-all-start = ((bf16[4,512,256]{2,1,0:T(8,128)(2,1)}), bf16[4,512,256]{2,1,0:T(8,128)(2,1)S(1)}, u32[]{:S(2)}, u32[]{:S(2)}) async-start(bf16[4,512,256]{2,1,0:T(8,128)(2,1)} %bitcast.20), calls=%async_computation | async-start | bytes 2097152 | tf_op jit(solution)/shard_map/all_to_all | solution.py:101
Sparse Core Ops, SparseCore 0:
  9.5 35.8 all-gather.12
  46.9 33.0 all-gather.14
  81.6 33.0 all-gather.10
  116.7 149.6 all-gather.26
  267.8 31.2 all-gather.16
  300.5 33.0 all-gather.24
  335.1 33.0 all-gather.22
  369.8 33.0 all-gather.20
  404.5 33.0 all-gather.18
  439.0 80.5 all-gather.28
where the time goes:
time: 533 us; the launch traced here: 532 us
  waiting for transfers between devices  400 us (75%)
  matrix products  68.2 us (13%)
  other arithmetic  32.4 us (6%)
  between operations  15 us (3%)
  local copies, waits for them, and re-layouts  9.29 us (2%)
    all_gather x1, waiting for transfers between devices, shards(): lax.all_gather(incoming, 'tensor', axis=3, tiled=True)[0, 0]  148 us
    all_gather x1, waiting for transfers between devices, shards(): context_whole = lax.all_gather(context, 'tensor', axis=1, tiled=True)  78.4 us
    all_gather x1, waiting for transfers between devices, shards(): lax.all_gather(m_value, 'dp', axis=1, tiled=True)  31.6 us
    all_gather x1, waiting for transfers between devices, shards(): lax.all_gather(v_value, 'dp', axis=1, tiled=True)  31.6 us
    sub x4, matrix products, one_block(): weights = jnp.exp(scores - highest)  31.5 us
    all_gather x1, waiting for transfers between devices, shards(): lax.all_gather(w_query, 'dp', axis=1, tiled=True)  30.9 us
    all_gather x1, waiting for transfers between devices, shards(): lax.all_gather(w_value, 'dp', axis=1, tiled=True)  30.9 us
    ppermute x1, waiting for transfers between devices, passed_along(): lax.ppermute(array, axis, [(i, (i + by) % count) for i in range(count)])  25.7 us
  transfers between devices with their start and end apart: 12, of which 9 were waited for; matrix products, arithmetic and copies ran while one was open for 19% of the time, Pallas kernels for 0%

commit v1 on v0

--- a/solution.py
+++ b/solution.py
@@ -97,7 +97,14 @@
     key_vals = projected[:, inner_local : 2 * inner_local].astype(jnp.bfloat16)
     value_vals = projected[:, 2 * inner_local :].astype(jnp.bfloat16)
     context = attend(queries, key_vals, value_vals, token_ids[0])
-    context_whole = lax.all_gather(context, "tensor", axis=1, tiled=True)
+    ring = [context]
+    for hop in range(3):
+        ring.append(lax.ppermute(ring[-1], "tensor", [(dev, (dev + 1) % 4) for dev in range(4)]))
+    context_whole = jnp.roll(
+        jnp.concatenate(ring[::-1], axis=1),
+        (lax.axis_index("tensor") + 1) * ring[0].shape[1],
+        axis=1,
+    )
     out_slice = lax.all_to_all(out_bf, "tensor", split_axis=0, concat_axis=1, tiled=True)
     update = lax.dot_general(
         context_whole, out_slice, (((1,), (1,)), ((), ())), preferred_element_type=jnp.float32

time: 533 us -> 458 us (0.86)
  waiting for transfers between devices: 400 us -> 319 us
    all_gather x1 -> x0, waiting for transfers between devices: 78.4 us -> none  [shards(): context_whole = lax.all_gather(context, 'tensor', axis=1, tiled=True)]
    ppermute x0 -> x3, waiting for transfers between devices: none -> 50.5 us  [shards(): lax.ppermute(ring[-1], 'tensor', [(dev, (dev + 1) % 4) for dev in range(4)])]
    all_gather x1, waiting for transfers between devices: 31.6 us -> 0.01 us  [shards(): lax.all_gather(v_value, 'dp', axis=1, tiled=True)]
    all_gather x1, waiting for transfers between devices: 14.6 us -> 0.01 us  [shards(): lax.all_gather(m_out, 'dp', axis=1, tiled=True)]
    all_gather x1, waiting for transfers between devices: 31.6 us -> 24.7 us  [shards(): lax.all_gather(m_value, 'dp', axis=1, tiled=True)]
  transfers between devices with their start and end apart: 12 -> 14, of which waited for: 9 -> 8; matrix products, arithmetic and copies ran while one was open for 19% -> 23% of each run, Pallas kernels for 0% -> 0%
where the time goes in v1:
time: 458 us; the launch traced here: 457 us
  waiting for transfers between devices  319 us (70%)
  matrix products  66 us (14%)
  other arithmetic  32.6 us (7%)
  between operations  14.7 us (3%)
  local copies, waits for them, and re-layouts  13.7 us (3%)
  starting transfers between devices  7.98 us (2%)
    all_gather x1, waiting for transfers between devices, shards(): lax.all_gather(incoming, 'tensor', axis=3, tiled=True)[0, 0]  148 us
    ppermute x3, waiting for transfers between devices, shards(): lax.ppermute(ring[-1], 'tensor', [(dev, (dev + 1) % 4) for dev in range(4)])  50.5 us
    sub x4, matrix products, one_block(): weights = jnp.exp(scores - highest)  31.5 us
    all_gather x1, waiting for transfers between devices, shards(): lax.all_gather(w_query, 'dp', axis=1, tiled=True)  30.9 us
    all_gather x1, waiting for transfers between devices, shards(): lax.all_gather(w_value, 'dp', axis=1, tiled=True)  30.9 us
    ppermute x1, waiting for transfers between devices, passed_along(): lax.ppermute(array, axis, [(i, (i + by) % count) for i in range(count)])  25.7 us
    all_gather x1, waiting for transfers between devices, shards(): lax.all_gather(m_value, 'dp', axis=1, tiled=True)  24.7 us
    dot_general x4, matrix products, one_block(): jnp.einsum('hqk,khd->qhd', probs, value_heads, preferred_element_type=jnp...  21.4 us
  transfers between devices with their start and end apart: 14, of which 8 were waited for; matrix products, arithmetic and copies ran while one was open for 23% of the time, Pallas kernels for 0%

profile of v1, /device:TPU:0, one launch (start us, length us, event | category | flops | bytes accessed | tf_op | source)
XLA Modules:
  0.0 456.9 jit_solution(10894581958008827759)
XLA Ops:
  9.5 25.7 %collective-permute-done = bf16[1,1,2048,512]{3,2,1,0:T(8,128)(2,1)S(1)} collective-permute-done((bf16[1,1,2048,512]{3,2,1,0:T(8,128)(2,1)}, bf16[1,1,2048,512]{3,2,1,0:T(8,128)(2,1)S(1)}, u32[]{:S(2)}, u32[]{:S(2)}) %collective-permute-start) | collective-permute-done | bytes 2097184 | tf_op jit(solution)/shard_map/ppermute | solution.py:14
  40.5 4.9 %all-gather.12.cloned.1.call-done = f32[1,2048,256]{2,1,0:T(8,128)} async-done(((f32[1,1024,256]{2,1,0:T(8,128)}), f32[1,2048,256]{2,1,0:T(8,128)}) %all-gather.12.cloned.1.call-update) | async-done | bytes 2097168 | tf_op jit(solution)/shard_map/all_gather | solution.py:74
  45.4 3.8 convert_bitcast_fusion.1
  49.2 30.9 %all-gather.14.cloned.1.call-done = f32[1,2048,256]{2,1,0:T(8,128)} async-done(((f32[1,1024,256]{2,1,0:T(8,128)}), f32[1,2048,256]{2,1,0:T(8,128)}) %all-gather.14.cloned.1.call-update) | async-done | bytes 2097168 | tf_op jit(solution)/shard_map/all_gather | solution.py:75
  80.0 3.8 convert_bitcast_fusion
  83.8 30.9 %all-gather.10.cloned.1.call-done = f32[1,2048,256]{2,1,0:T(8,128)} async-done(((f32[1,1024,256]{2,1,0:T(8,128)}), f32[1,2048,256]{2,1,0:T(8,128)}) %all-gather.10.cloned.1.call-update) | async-done | bytes 2097168 | tf_op jit(solution)/shard_map/all_gather | solution.py:73
  114.7 4.1 convert_bitcast_fusion.2
  118.8 147.5 %all-gather.26.cloned.1.call-done = bf16[1,1,2048,2048]{3,2,1,0:T(8,128)(2,1)} async-done(((bf16[1,1,2048,512]{3,2,1,0:T(8,128)(2,1)}), bf16[1,1,2048,2048]{3,2,1,0:T(8,128)(2,1)}) %all-gather.26.cloned.1.call-update) | async-done | bytes 8388624 | tf_op jit(solution)/shard_map/all_gather | solution.py:92
  266.4 9.4 %fusion.23 = bf16[2048,768]{0,1:T(8,128)(2,1)S(1)} fusion(bf16[1,1,2048,2048]{3,2,1,0:T(8,128)(2,1)} %all-gather.26.cloned.1.call-done, bf16[2048,256]{1,0:T(8,128)(2,1)S(1)} %get-tuple-element.124, bf16[2048,256]{1,0:T(8,128)(2,1)S(1)} %get-tuple-element.122, bf16[2048,256]{1,0:T(8,128)(2,1)} %get-tuple-element.120), kind=kOutput, calls=%fused_computation.26 | convolution fusion | flops 6453460992 | bytes 14680064 | tf_op jit(solution)/shard_map/dot_general | solution.py:91
  278.4 63.1 %while.11 = (s32[]{:T(128)}, bf16[4,512,256]{2,1,0:T(8,128)(2,1)S(1)}, s32[2048]{0:T(1024)S(1)}, s32[4]{0:T(128)S(1)}, s32[2048]{0:T(1024)S(1)}, /*index=5*/bf16...) while((s32[]{:T(128)}, ...), condition=%wide.region_5.6_spmd.clone, body=%wide.region_2.5_spmd.clone.sunk | while | flops 1089603584 | bytes 23105728 | solution.py:53
  280.7 7.9 %fusion.56 = (f32[2,512]{1,0:T(2,128)S(1)}, f32[2,512,2048]{2,1,0:T(8,128)}) fusion(pred[512,2048]{1,0:T(8,128)(4,1)S(1)} %compare_and_fusion.2, bf16[512,2,128]{0,2,1:T(8,128)(2,1)S(1)} %bitcast.70, bf16[2048,2,128]{2,0,1:T(8,128)(2,1)} %get-tuple-element.211), kind=kOutput, calls=%fused_computation.54.clone.1 | convolution fusion | flops 545261568 | bytes 10752000 | tf_op jit(solution)/shard_map/while/body/eval_jaxpr/sub | solution.py:46
  288.6 5.2 %fusion.57 = bf16[2,512,128]{1,2,0:T(8,128)(2,1)S(1)} fusion(bf16[2048,2,128]{0,2,1:T(8,128)(2,1)} %get-tuple-element.212, f32[2,512,2048]{2,1,0:T(8,128)} %get-tuple-element.179, f32[2,512]{1,0:T(2,128)S(1)} %get-tuple-element.180), kind=kOutput, calls=%fused_computation.10.clone.1 | convolution fusion | flops 541196288 | bytes 9703424 | tf_op jit(solution)/shard_map/while/body/eval_jaxpr/hqk,khd->qhd/dot_general | solution.py:48
  296.4 7.9 %fusion.56 = (f32[2,512]{1,0:T(2,128)S(1)}, f32[2,512,2048]{2,1,0:T(8,128)}) fusion(pred[512,2048]{1,0:T(8,128)(4,1)S(1)} %compare_and_fusion.2, bf16[512,2,128]{0,2,1:T(8,128)(2,1)S(1)} %bitcast.70, bf16[2048,2,128]{2,0,1:T(8,128)(2,1)} %get-tuple-element.211), kind=kOutput, calls=%fused_computation.54.clone.1 | convolution fusion | flops 545261568 | bytes 10752000 | tf_op jit(solution)/shard_map/while/body/eval_jaxpr/sub | solution.py:46
  304.2 5.7 %fusion.57 = bf16[2,512,128]{1,2,0:T(8,128)(2,1)S(1)} fusion(bf16[2048,2,128]{0,2,1:T(8,128)(2,1)} %get-tuple-element.212, f32[2,512,2048]{2,1,0:T(8,128)} %get-tuple-element.179, f32[2,512]{1,0:T(2,128)S(1)} %get-tuple-element.180), kind=kOutput, calls=%fused_computation.10.clone.1 | convolution fusion | flops 541196288 | bytes 9703424 | tf_op jit(solution)/shard_map/while/body/eval_jaxpr/hqk,khd->qhd/dot_general | solution.py:48
  312.5 7.9 %fusion.56 = (f32[2,512]{1,0:T(2,128)S(1)}, f32[2,512,2048]{2,1,0:T(8,128)}) fusion(pred[512,2048]{1,0:T(8,128)(4,1)S(1)} %compare_and_fusion.2, bf16[512,2,128]{0,2,1:T(8,128)(2,1)S(1)} %bitcast.70, bf16[2048,2,128]{2,0,1:T(8,128)(2,1)} %get-tuple-element.211), kind=kOutput, calls=%fused_computation.54.clone.1 | convolution fusion | flops 545261568 | bytes 10752000 | tf_op jit(solution)/shard_map/while/body/eval_jaxpr/sub | solution.py:46
  320.4 5.2 %fusion.57 = bf16[2,512,128]{1,2,0:T(8,128)(2,1)S(1)} fusion(bf16[2048,2,128]{0,2,1:T(8,128)(2,1)} %get-tuple-element.212, f32[2,512,2048]{2,1,0:T(8,128)} %get-tuple-element.179, f32[2,512]{1,0:T(2,128)S(1)} %get-tuple-element.180), kind=kOutput, calls=%fused_computation.10.clone.1 | convolution fusion | flops 541196288 | bytes 9703424 | tf_op jit(solution)/shard_map/while/body/eval_jaxpr/hqk,khd->qhd/dot_general | solution.py:48
  328.2 7.9 %fusion.56 = (f32[2,512]{1,0:T(2,128)S(1)}, f32[2,512,2048]{2,1,0:T(8,128)}) fusion(pred[512,2048]{1,0:T(8,128)(4,1)S(1)} %compare_and_fusion.2, bf16[512,2,128]{0,2,1:T(8,128)(2,1)S(1)} %bitcast.70, bf16[2048,2,128]{2,0,1:T(8,128)(2,1)} %get-tuple-element.211), kind=kOutput, calls=%fused_computation.54.clone.1 | convolution fusion | flops 545261568 | bytes 10752000 | tf_op jit(solution)/shard_map/while/body/eval_jaxpr/sub | solution.py:46
  336.0 5.2 %fusion.57 = bf16[2,512,128]{1,2,0:T(8,128)(2,1)S(1)} fusion(bf16[2048,2,128]{0,2,1:T(8,128)(2,1)} %get-tuple-element.212, f32[2,512,2048]{2,1,0:T(8,128)} %get-tuple-element.179, f32[2,512]{1,0:T(2,128)S(1)} %get-tuple-element.180), kind=kOutput, calls=%fused_computation.10.clone.1 | convolution fusion | flops 541196288 | bytes 9703424 | tf_op jit(solution)/shard_map/while/body/eval_jaxpr/hqk,khd->qhd/dot_general | solution.py:48
  341.8 4.4 fusion.41
  346.2 5.1 %all-to-all-start = ((bf16[4,512,256]{2,1,0:T(8,128)(2,1)}), bf16[4,512,256]{2,1,0:T(8,128)(2,1)}, u32[]{:S(2)}, u32[]{:S(2)}) async-start(bf16[4,512,256]{2,1,0:T(8,128)(2,1)} %bitcast.20), calls=%async_computation | async-start | bytes 2097152 | tf_op jit(solution)/shard_map/all_to_all | solution.py:108
  351.3 18.3 %collective-permute-done.1 = bf16[2048,256]{1,0:T(8,128)(2,1)S(1)} collective-permute-done((bf16[2048,256]{1,0:T(8,128)(2,1)S(1)}, bf16[2048,256]{1,0:T(8,128)(2,1)S(1)}, u32[]{:S(2)}, u32[]{:S(2)}) %collective-permute-start.1) | collective-permute-done | bytes 1048608 | tf_op jit(solution)/shard_map/ppermute | solution.py:102
  375.7 32.2 %collective-permute-done.2 = bf16[2048,256]{1,0:T(8,128)(2,1)S(1)} collective-permute-done((bf16[2048,256]{1,0:T(8,128)(2,1)S(1)}, bf16[2048,256]{1,0:T(8,128)(2,1)S(1)}, u32[]{:S(2)}, u32[]{:S(2)}) %collective-permute-start.2) | collective-permute-done | bytes 1048608 | tf_op jit(solution)/shard_map/ppermute | solution.py:102
  412.9 24.7 %all-gather.18.cloned.1.call-done = f32[1,2048,256]{2,1,0:T(8,128)} async-done(((f32[1,1024,256]{2,1,0:T(8,128)}), f32[1,2048,256]{2,1,0:T(8,128)}) %all-gather.18.cloned.1.call-update) | async-done | bytes 2097168 | tf_op jit(solution)/shard_map/all_gather | solution.py:77
  446.7 3.7 fusion.34
  (86 shorter events, 37.1 us)
Async XLA Ops:
  7.2 38.2 %all-gather.12.cloned.1.call-start = ((), (), s32[]{:S(2)}) async-start(), calls=%async_computation.2 | async-start | bytes 3145728 | tf_op jit(solution)/shard_map/all_gather | solution.py:74
  7.9 32.0 %copy-start.2 = (s32[1,2048]{1,0:T(1,128)S(1)}, s32[1,2048]{1,0:T(1,128)}, u32[]{:S(2)}) copy-start(s32[1,2048]{1,0:T(1,128)} %param.14) | copy-start | bytes 24580
  7.9 72.1 %all-gather.14.cloned.1.call-start = ((), (), s32[]{:S(2)}) async-start(), calls=%async_computation.3 | async-start | bytes 3145728 | tf_op jit(solution)/shard_map/all_gather | solution.py:75
  8.7 106.0 %all-gather.10.cloned.1.call-start = ((), (), s32[]{:S(2)}) async-start(), calls=%async_computation.1 | async-start | bytes 3145728 | tf_op jit(solution)/shard_map/all_gather | solution.py:73
  8.7 26.4 %collective-permute-start = (bf16[1,1,2048,512]{3,2,1,0:T(8,128)(2,1)}, bf16[1,1,2048,512]{3,2,1,0:T(8,128)(2,1)S(1)}, u32[]{:S(2)}, u32[]{:S(2)}) collective-permute-start(bf16[1,1,2048,512]{3,2,1,0:T(8,128)(2,1)} %param.15), channel_id=1, source_target_pairs={{0,4},{4,8},{8,12},{12,0},{1,5},{5,9},{9,13},{13,1},{2,6},{6,10},{... | collective-permute-start | bytes 6291464 | tf_op jit(solution)/shard_map/ppermute | solution.py:14
  9.4 257.0 %all-gather.26.cloned.1.call-start = ((), (), s32[]{:S(2)}) async-start(), calls=%async_computation.9 | async-start | bytes 10485760 | tf_op jit(solution)/shard_map/all_gather | solution.py:92
  35.1 1.3 copy-start
  36.5 305.3 %all-gather.16.cloned.1.call-start = ((), (), s32[]{:S(2)}) async-start(), calls=%async_computation.4 | async-start | bytes 3145728 | tf_op jit(solution)/shard_map/all_gather | solution.py:76
  37.1 332.5 %all-gather.24.cloned.1.call-start = ((), (), s32[]{:S(2)}) async-start(), calls=%async_computation.8 | async-start | bytes 3145728 | tf_op jit(solution)/shard_map/all_gather | solution.py:80
  37.6 335.0 %all-gather.22.cloned.1.call-start = ((), (), s32[]{:S(2)}) async-start(), calls=%async_computation.7 | async-start | bytes 3145728 | tf_op jit(solution)/shard_map/all_gather | solution.py:79
  38.4 371.3 %all-gather.20.cloned.1.call-start = ((), (), s32[]{:S(2)}) async-start(), calls=%async_computation.6 | async-start | bytes 3145728 | tf_op jit(solution)/shard_map/all_gather | solution.py:78
  39.1 398.5 %all-gather.18.cloned.1.call-start = ((), (), s32[]{:S(2)}) async-start(), calls=%async_computation.5 | async-start | bytes 3145728 | tf_op jit(solution)/shard_map/all_gather | solution.py:77
  341.4 28.2 %collective-permute-start.1 = (bf16[2048,256]{1,0:T(8,128)(2,1)S(1)}, bf16[2048,256]{1,0:T(8,128)(2,1)S(1)}, u32[]{:S(2)}, u32[]{:S(2)}) collective-permute-start(bf16[2048,256]{1,0:T(8,128)(2,1)S(1)} %bitcast.72), channel_id=1, source_target_pairs={{0,1},{1,2},{2,3},{3,0},{4,5},{5,6},{6,7},{7,4},{8,9},{9,10},{10,1... | collective-permute-start | bytes 3145736 | tf_op jit(solution)/shard_map/ppermute | solution.py:102
  346.2 94.4 %all-to-all-start = ((bf16[4,512,256]{2,1,0:T(8,128)(2,1)}), bf16[4,512,256]{2,1,0:T(8,128)(2,1)}, u32[]{:S(2)}, u32[]{:S(2)}) async-start(bf16[4,512,256]{2,1,0:T(8,128)(2,1)} %bitcast.20), calls=%async_computation | async-start | bytes 2097152 | tf_op jit(solution)/shard_map/all_to_all | solution.py:108
  369.6 38.3 %collective-permute-start.2 = (bf16[2048,256]{1,0:T(8,128)(2,1)S(1)}, bf16[2048,256]{1,0:T(8,128)(2,1)S(1)}, u32[]{:S(2)}, u32[]{:S(2)}) collective-permute-start(bf16[2048,256]{1,0:T(8,128)(2,1)S(1)} %collective-permute-done.1), channel_id=1, source_target_pairs={{0,1},{1,2},{2,3},{3,0},{4,5},{5,6},{6,7},{7,4},{8,9},{9,10},{10,1... | collective-permute-start | bytes 3145736 | tf_op jit(solution)/shard_map/ppermute | solution.py:102
  407.9 35.0 %collective-permute-start.3 = (bf16[2048,256]{1,0:T(8,128)(2,1)S(1)}, bf16[2048,256]{1,0:T(8,128)(2,1)}, u32[]{:S(2)}, u32[]{:S(2)}) collective-permute-start(bf16[2048,256]{1,0:T(8,128)(2,1)S(1)} %collective-permute-done.2), channel_id=1, source_target_pairs={{0,1},{1,2},{2,3},{3,0},{4,5},{5,6},{6,7},{7,4},{8,9},{9,10},{10,1... | collective-permute-start | bytes 3145736 | tf_op jit(solution)/shard_map/ppermute | solution.py:102
  444.7 1.9 copy-start.1
Sparse Core Ops, SparseCore 0:
  9.5 35.8 all-gather.11
  46.9 33.0 all-gather.13
  81.6 33.0 all-gather.9
  116.7 149.6 all-gather.25
  267.8 31.2 all-gather.15
  300.5 33.0 all-gather.23
  335.1 33.0 all-gather.21
  369.8 33.0 all-gather.19
  404.5 33.0 all-gather.17
